TPU v7x, 32 devices: a whole 2x2x4 slice. The times are simulated.
32 devices in a mesh: vpair: 4 (over y, x), rank: 8 (over z, core).
Axes of the slice: x: 2, y: 2, z: 4, core: 2. Of those that a mesh axis runs over, the one named last changes fastest.
Arguments:
- amplitudes: bfloat16 [8, 1200, 1200], P(None, 'vpair', 'rank'), may hold values from -6 to 6
- factors: bfloat16 [1200, 8192], P('vpair', 'rank'), may hold values from -0.1875 to 0.1875
- kernel: bfloat16 [8192, 8192], P('vpair', 'rank'), may hold values from -0.875 to 0.875
- other_terms: float32 [8, 1200, 1200], P(None, 'vpair'), may hold values from -6 to 6
- virt_energy: float32 [1200], replicated, may hold values from 0.2 to 4
- pair_energy: float32 [8], replicated, may hold values from -3 to -0.5
Outputs:
- residual: float32 [8, 1200, 1200], P(None, 'vpair')
- update_rms: float32 [], replicated
All inputs are finite; a program needn't handle non-finite values.
Results may differ from a plain program's by a relative error of at most 0.0035.
Values may be sent and summed in bfloat16 or wider, within the bound.
A program may use at most 192 MiB of HBM per device.

v0:
```python
import jax
import jax.numpy as jnp
from jax import lax
from jax.sharding import PartitionSpec as P

epsilon = 1e-06


def shards(amplitudes, factors, kernel, other_terms, virt_energy, pair_energy):
    vpair_count = lax.axis_size("vpair")
    pair_count = amplitudes.shape[0]
    row_block = amplitudes.shape[1]
    col_block = amplitudes.shape[2]
    virt_count = row_block * vpair_count
    right_block = kernel.shape[1]
    factor_rows = lax.all_gather(factors, "rank", axis=1, tiled=True)
    factor_full = lax.all_gather(factor_rows, "vpair", axis=0, tiled=True)
    factor_cols = lax.dynamic_slice_in_dim(
        factor_full, lax.axis_index("rank") * right_block, right_block, 1
    )
    half_done = jnp.einsum(
        "ons,sh->onh",
        lax.all_gather(amplitudes, "rank", axis=2, tiled=True),
        factor_cols,
        preferred_element_type=jnp.float32,
    ).astype(jnp.bfloat16)
    kernel_sub = lax.all_to_all(kernel, "vpair", split_axis=1, concat_axis=0, tiled=True).astype(
        jnp.float32
    )
    coupled = jnp.einsum(
        "cp,icq->ipq",
        factor_full,
        lax.all_to_all(half_done, "vpair", split_axis=2, concat_axis=1, tiled=True),
        preferred_element_type=jnp.float32,
    )
    weighted = (kernel_sub[None] * coupled).astype(jnp.bfloat16)
    ladder_half = jnp.einsum(
        "ap,ipq->iaq", factor_full, weighted, preferred_element_type=jnp.float32
    ).astype(jnp.bfloat16)
    back_half = lax.all_to_all(ladder_half, "vpair", split_axis=1, concat_axis=2, tiled=True)
    partial_value = jnp.einsum(
        "iaq,bq->iab", back_half, factor_cols, preferred_element_type=jnp.float32
    )
    row_energy = lax.dynamic_slice_in_dim(
        virt_energy, lax.axis_index("vpair") * row_block, row_block, 0
    )
    ladder_share = lax.psum_scatter(partial_value, "rank", scatter_dimension=2, tiled=True)
    col_start = lax.axis_index("rank") * col_block
    own_terms = lax.dynamic_slice_in_dim(other_terms, col_start, col_block, 2)
    part_residual = own_terms + ladder_share
    col_energy = lax.dynamic_slice_in_dim(virt_energy, col_start, col_block, 0)
    denominator = row_energy[None, :, None] + col_energy[None, None, :] - pair_energy[:, None, None]
    update = part_residual / denominator
    squares = lax.psum(jnp.sum(update * update), ("vpair", "rank"))
    residual = lax.all_gather(part_residual, "rank", axis=2, tiled=True)
    update_rms = jnp.sqrt(squares / (pair_count * virt_count * virt_count) + epsilon)
    return (residual, update_rms)


def solution(mesh):
    placed = (
        P(None, "vpair", "rank"),
        P("vpair", "rank"),
        P("vpair", "rank"),
        P(None, "vpair", None),
        P(),
        P(),
    )
    return jax.shard_map(
        shards, mesh=mesh, in_specs=placed, out_specs=(P(None, "vpair", None), P()), check_vma=False
    )
```

profile of v0, /device:TPU:0, one launch (start us, length us, event | category | flops | bytes accessed | tf_op | source)
XLA Modules:
  0.0 988.1 jit_solution(17243260461475593939)
XLA Ops:
  7.9 58.1 %all-gather.6.cloned.1.call-done = bf16[300,8192]{1,0:T(8,128)(2,1)} async-done(((bf16[300,1024]{1,0:T(8,128)(2,1)}), bf16[300,8192]{1,0:T(8,128)(2,1)}) %all-gather.6.cloned.1.call-update) | async-done | bytes 4915216 | tf_op jit(solution)/shard_map/all_gather | solution.py:16
  66.8 6.6 copy.34
  73.4 5.2 all-to-all-start
  78.6 213.5 %all-gather.12.cloned.1.call-done = bf16[4,300,8192]{2,1,0:T(8,128)(2,1)} async-done(((bf16[1,300,8192]{2,1,0:T(8,128)(2,1)}), bf16[4,300,8192]{2,1,0:T(8,128)(2,1)}) %all-gather.12.cloned.1.call-update) | async-done | bytes 19660816 | tf_op jit(solution)/shard_map/all_gather | solution.py:17
  292.1 20.4 %reshape.49 = bf16[1200,8192]{1,0:T(8,128)(2,1)} reshape(bf16[4,300,8192]{2,1,0:T(8,128)(2,1)} %all-gather.12.cloned.1.call-done) | data formatting | bytes 39321600
  312.5 54.9 %all-gather.8.cloned.1.call-done = bf16[8,300,1200]{1,0,2:T(8,128)(2,1)} async-done(((bf16[8,300,150]{1,0,2:T(8,128)(2,1)}), bf16[8,300,1200]{1,0,2:T(8,128)(2,1)}) %all-gather.8.cloned.1.call-update) | async-done | bytes 5760016 | tf_op jit(solution)/shard_map/all_gather | solution.py:23
  367.5 12.2 %convert_bitcast_fusion.1 = bf16[8,300,1024]{2,1,0:T(8,128)(2,1)} fusion(bf16[8,300,1200]{1,0,2:T(8,128)(2,1)} %all-gather.8.cloned.1.call-done, bf16[1200,8192]{1,0:T(8,128)(2,1)} %reshape.49, s32[]{:T(128)S(6)} %select_n.11), kind=kOutput, calls=%fused_computation.9 | convolution fusion | flops 5900697600 | bytes 14745604 | tf_op jit(solution)/shard_map/ons,sh->onh/dot_general | solution.py:21
  379.7 8.6 copy.38
  388.3 5.2 all-to-all-start.1
  393.9 6.7 convert_bitcast_fusion
  400.6 8.7 copy.35
  409.3 8.9 copy.36
  418.2 19.5 %reshape.51 = bf16[1200,8192,1]{1,0,2:T(8,128)(2,1)} reshape(bf16[4,300,8192]{2,1,0:T(8,128)(2,1)} %all-gather.12.cloned.1.call-done) | data formatting | bytes 39321600
  437.7 26.5 %all-to-all-done.1 = bf16[8,300,1024]{1,0,2:T(8,128)(2,1)} async-done(((bf16[8,300,1024]{1,0,2:T(8,128)(2,1)}), bf16[8,300,1024]{1,0,2:T(8,128)(2,1)}, u32[]{:S(2)}, u32[]{:S(2)}) %all-to-all-start.1) | async-done | bytes 4915232 | tf_op jit(solution)/shard_map/all_to_all | solution.py:33
  464.1 12.8 %copy.51 = bf16[8,300,4,256]{3,2,0,1:T(4,128)(2,1)} copy(bf16[8,300,4,256]{1,0,3,2:T(8,128)(2,1)} %bitcast.6) | data formatting | bytes 9830400 | tf_op jit(solution)/shard_map/all_to_all | solution.py:33
  476.9 5.2 copy.40
  482.2 54.1 %fusion.39 = bf16[8,8192,256]{1,2,0:T(8,128)(2,1)} fusion(f32[8192,256]{0,1:T(8,128)} %copy.36, bf16[1200,8192,1]{1,0,2:T(8,128)(2,1)} %reshape.51, bf16[8,1200,256]{2,0,1:T(8,128)(2,1)} %bitcast.49), kind=kOutput, calls=%fused_computation.1.clone.clone.clone.clone.clone.clone.1 | convolution fusion | flops 40298872832 | bytes 66519040 | tf_op jit(solution)/shard_map/cp,icq->ipq/dot_general | solution.py:30
  536.2 51.8 %fusion.13 = bf16[8,1200,256]{2,1,0:T(8,128)(2,1)} fusion(bf16[1200,8192,1]{1,0,2:T(8,128)(2,1)} %reshape.51, bf16[8,8192,256]{1,2,0:T(8,128)(2,1)} %fusion.39), kind=kOutput, calls=%fused_computation.11 | convolution fusion | flops 40267776000 | bytes 58130432 | tf_op jit(solution)/shard_map/ap,ipq->iaq/dot_general | solution.py:37
  588.0 8.8 copy.43
  596.8 58.1 %all_to_all.49 = bf16[8,1200,256]{2,0,1:T(8,128)(2,1)S(1)} all-to-all(bf16[8,1200,256]{2,0,1:T(8,128)(2,1)S(1)} %copy.43), channel_id=1, replica_groups=mesh['vpair'=4,'rank'=8] {'vpair'}, dimensions={1} | all-to-all | bytes 9830400 | tf_op jit(solution)/shard_map/all_to_all | solution.py:40
  654.9 0.7 copy.55
  655.6 10.7 %fusion.20 = f32[8,300,1200]{2,0,1:T(8,128)} fusion(bf16[8,300,1024]{2,0,1:T(8,128)(2,1)S(1)} %bitcast.48, bf16[1200,8192]{1,0:T(8,128)(2,1)} %reshape.49, s32[]{:T(128)S(6)} %select_n.11), kind=kOutput, calls=%fused_computation.12 | convolution fusion | flops 5898240000 | bytes 18892804 | tf_op jit(solution)/shard_map/iaq,bq->iab/dot_general | solution.py:41
  666.3 14.2 %copy.46 = f32[8,300,1200]{1,0,2:T(8,128)} copy(f32[8,300,1200]{2,0,1:T(8,128)} %fusion.20) | data formatting | bytes 23040000 | tf_op jit(solution)/shard_map/iaq,bq->iab/dot_general | solution.py:41
  680.6 0.8 dynamic_slice.15
  681.3 0.8 dynamic_slice.14
  682.1 3.5 constant_dynamic-slice_fusion
  685.6 1.9 copy.54
  687.6 139.6 %reduce-scatter.2.cloned.1.call-done = f32[8,300,150]{1,0,2:T(8,128)} async-done(((f32[8,300,1200]{1,0,2:T(8,128)}), f32[8,300,150]{1,0,2:T(8,128)}) %reduce-scatter.2.cloned.1.call-update) | async-done | bytes 1440016 | tf_op jit(solution)/shard_map/reduce_scatter | solution.py:47
  827.1 4.3 multiply_reduce_fusion
  831.5 43.4 %psum.7 = f32[]{:T(128)} all-reduce(f32[]{:T(128)} %get-tuple-element.10), channel_id=1, replica_groups=mesh['vpair'=4,'rank'=8] {'vpair','rank'}, use_global_device_ids=true, to_apply=%region_2.0 | all-reduce | flops 1 | bytes 8 | tf_op jit(solution)/shard_map/psum | solution.py:54
  875.5 90.0 %all-gather.10.cloned.1.call-done = f32[8,300,1200]{1,0,2:T(8,128)} async-done(((f32[8,300,150]{1,0,2:T(8,128)}), f32[8,300,1200]{1,0,2:T(8,128)}) %all-gather.10.cloned.1.call-update) | async-done | bytes 11520016 | tf_op jit(solution)/shard_map/all_gather | solution.py:55
  965.5 14.7 %copy.47 = f32[8,300,1200]{2,0,1:T(8,128)} copy(f32[8,300,1200]{1,0,2:T(8,128)} %all-gather.10.cloned.1.call-done) | data formatting | bytes 23040000
  (14 shorter events, 2.0 us)
Async XLA Ops:
  7.2 58.9 %all-gather.6.cloned.1.call-start = ((), (), s32[]{:S(2)}) async-start(), calls=%async_computation.4 | async-start | bytes 5603328 | tf_op jit(solution)/shard_map/all_gather | solution.py:16
  7.9 284.2 %all-gather.12.cloned.1.call-start = ((), (), s32[]{:S(2)}) async-start(), calls=%async_computation.8 | async-start | bytes 24903680 | tf_op jit(solution)/shard_map/all_gather | solution.py:17
  66.1 301.4 %all-gather.8.cloned.1.call-start = ((), (), s32[]{:S(2)}) async-start(), calls=%async_computation.5 | async-start | bytes 8294400 | tf_op jit(solution)/shard_map/all_gather | solution.py:23
  73.4 314.9 %all-to-all-start = ((bf16[2048,4,256]{0,2,1:T(8,128)(2,1)}), bf16[2048,4,256]{0,2,1:T(8,128)(2,1)}, u32[]{:S(2)}, u32[]{:S(2)}) async-start(bf16[2048,4,256]{0,2,1:T(8,128)(2,1)} %bitcast.46), calls=%async_computation | async-start | bytes 8388608 | tf_op jit(solution)/shard_map/all_to_all | solution.py:27
  388.3 75.8 %all-to-all-start.1 = ((bf16[8,300,1024]{1,0,2:T(8,128)(2,1)}), bf16[8,300,1024]{1,0,2:T(8,128)(2,1)}, u32[]{:S(2)}, u32[]{:S(2)}) async-start(bf16[8,300,1024]{1,0,2:T(8,128)(2,1)} %copy.38), calls=%async_computation.1 | async-start | bytes 12582912 | tf_op jit(solution)/shard_map/all_to_all | solution.py:33
  393.6 433.6 %reduce-scatter.2.cloned.1.call-start = ((), (), s32[]{:S(2)}) async-start(), calls=%async_computation.6 | async-start | bytes 16588800 | tf_op jit(solution)/shard_map/reduce_scatter | solution.py:47
  680.5 146.6 %copy-start = (f32[8]{0:T(128)S(1)}, f32[8]{0:T(128)}, u32[]{:S(2)}) copy-start(f32[8]{0:T(128)} %param.11) | copy-start | bytes 100
  680.5 285.0 %all-gather.10.cloned.1.call-start = ((), (), s32[]{:S(2)}) async-start(), calls=%async_computation.7 | async-start | bytes 16588800 | tf_op jit(solution)/shard_map/all_gather | solution.py:55
Sparse Core Ops, SparseCore 0:
  9.6 56.4 all-gather.5
  67.9 224.1 all-gather.11
  293.8 73.6 all-gather.7
  680.6 146.4 reduce-scatter.1
  831.6 133.8 all-gather.9
where the time goes:
time: 995 us; the launch traced here: 988 us
  waiting for transfers between devices  584 us (59%)
  local copies, waits for them, and re-layouts  136 us (14%)
  matrix products  129 us (13%)
  blocking collectives  102 us (10%)
  between operations  15.9 us (2%)
  other arithmetic  11 us (1%)
  starting transfers between devices  10.9 us (1%)
    all_gather x1, waiting for transfers between devices, shards(): factor_full = lax.all_gather(factor_rows, 'vpair', axis=0, tiled=True)  214 us
    reduce_scatter x1, waiting for transfers between devices, shards(): lax.psum_scatter(partial_value, 'rank', scatter_dimension=2, tiled=True)  140 us
    all_gather x1, waiting for transfers between devices, shards(): residual = lax.all_gather(part_residual, 'rank', axis=2, tiled=True)  90 us
    unnamed x7, local copies, waits for them, and re-layouts  63 us
    all_gather x1, waiting for transfers between devices, shards(): factor_rows = lax.all_gather(factors, 'rank', axis=1, tiled=True)  58.1 us
    all_to_all x1, blocking collectives, shards(): lax.all_to_all(ladder_half, 'vpair', split_axis=1, concat_axis=2, tiled=T...  58.1 us
    all_gather x1, waiting for transfers between devices, shards(): lax.all_gather(amplitudes, 'rank', axis=2, tiled=True)  54.9 us
    dot_general x1, matrix products, shards(): jnp.einsum('cp,icq->ipq', factor_full, lax.all_to_all(half_done, 'vpair',...  54.1 us
  transfers between devices with their start and end apart: 7, of which 6 were waited for; matrix products, arithmetic and copies ran while one was open for 10% of the time, Pallas kernels for 0%

commit v1 on v0

--- a/solution.py
+++ b/solution.py
@@ -18,11 +18,35 @@
     factor_cols = lax.dynamic_slice_in_dim(
         factor_full, lax.axis_index("rank") * right_block, right_block, 1
     )
-    half_done = jnp.einsum(
-        "ons,sh->onh",
-        lax.all_gather(amplitudes, "rank", axis=2, tiled=True),
-        factor_cols,
-        preferred_element_type=jnp.float32,
+
+    def expand_the_frame(field, on_dim, block_here):
+        q_next = jax.lax.axis_index("rank")
+        odd = jax.lax.axis_size("rank")
+        tall, out_arr = (odd, q_next)
+        seen = []
+        to_i = 0
+        while to_i < tall:
+            seen.append((to_i, (to_i - 1) % tall))
+            to_i += 1
+        tile_out = field.shape[on_dim]
+        side_arr = field
+        w1 = block_here(side_arr, out_arr * tile_out)
+        b = 1
+        while b < tall:
+            side_arr = jax.lax.ppermute(side_arr, "rank", seen)
+            w1 = w1 + block_here(side_arr, (out_arr + b) % tall * tile_out)
+            b += 1
+        return w1
+
+    half_done = expand_the_frame(
+        amplitudes,
+        2,
+        lambda own_block, start: jnp.einsum(
+            "ons,sh->onh",
+            own_block,
+            lax.dynamic_slice_in_dim(factor_cols, start, own_block.shape[2], axis=0),
+            preferred_element_type=jnp.float32,
+        ),
     ).astype(jnp.bfloat16)
     kernel_sub = lax.all_to_all(kernel, "vpair", split_axis=1, concat_axis=0, tiled=True).astype(
         jnp.float32

time: 995 us -> 995 us (level)
  waiting for transfers between devices: 584 us -> 511 us
  matrix products: 129 us -> 181 us
  starting transfers between devices: 10.9 us -> 32.9 us
    all_gather x1, waiting for transfers between devices: 214 us -> 139 us  [shards(): factor_full = lax.all_gather(factor_rows, 'vpair', axis=0, tiled=True)]
    ppermute x0 -> x7, waiting for transfers between devices: none -> 55.1 us  [expand_the_frame(): side_arr = jax.lax.ppermute(side_arr, 'rank', seen)]
    all_gather x1 -> x0, waiting for transfers between devices: 54.9 us -> none  [shards(): lax.all_gather(amplitudes, 'rank', axis=2, tiled=True)]
    dot_general x1 -> x8, matrix products: 12.2 us -> 64.7 us  [shards(): jnp.einsum('ons,sh->onh', own_block, lax.dynamic_slice_in_dim(factor_cols...]
    ppermute x0 -> x7, starting transfers between devices: none -> 22.2 us  [expand_the_frame(): side_arr = jax.lax.ppermute(side_arr, 'rank', seen)]
    unnamed x7 -> x17, local copies, waits for them, and re-layouts: 63 us -> 64.8 us
  transfers between devices with their start and end apart: 7 -> 13, of which waited for: 6 -> 10; matrix products, arithmetic and copies ran while one was open for 10% -> 15% of each run, Pallas kernels for 0% -> 0%
where the time goes in v1:
time: 995 us; the launch traced here: 990 us
  waiting for transfers between devices  511 us (51%)
  matrix products  181 us (18%)
  local copies, waits for them, and re-layouts  137 us (14%)
  blocking collectives  101 us (10%)
  starting transfers between devices  32.9 us (3%)
  between operations  16 us (2%)
  other arithmetic  11 us (1%)
    reduce_scatter x1, waiting for transfers between devices, shards(): lax.psum_scatter(partial_value, 'rank', scatter_dimension=2, tiled=True)  143 us
    all_gather x1, waiting for transfers between devices, shards(): factor_full = lax.all_gather(factor_rows, 'vpair', axis=0, tiled=True)  139 us
    all_gather x1, waiting for transfers between devices, shards(): residual = lax.all_gather(part_residual, 'rank', axis=2, tiled=True)  90 us
    unnamed x17, local copies, waits for them, and re-layouts  64.8 us
    dot_general x8, matrix products, shards(): jnp.einsum('ons,sh->onh', own_block, lax.dynamic_slice_in_dim(factor_cols...  64.7 us
    all_gather x1, waiting for transfers between devices, shards(): factor_rows = lax.all_gather(factors, 'rank', axis=1, tiled=True)  58.1 us
    all_to_all x1, blocking collectives, shards(): lax.all_to_all(ladder_half, 'vpair', split_axis=1, concat_axis=2, tiled=T...  57.8 us
    ppermute x7, waiting for transfers between devices, expand_the_frame(): side_arr = jax.lax.ppermute(side_arr, 'rank', seen)  55.1 us
  transfers between devices with their start and end apart: 13, of which 10 were waited for; matrix products, arithmetic and copies ran while one was open for 15% of the time, Pallas kernels for 0%

profile of v1, /device:TPU:0, one launch (start us, length us, event | category | flops | bytes accessed | tf_op | source)
XLA Modules:
  0.0 990.0 jit_solution(16813119738426380797)
XLA Ops:
  7.9 58.1 %all-gather.5.cloned.1.call-done = bf16[300,8192]{1,0:T(8,128)(2,1)} async-done(((bf16[300,1024]{1,0:T(8,128)(2,1)}), bf16[300,8192]{1,0:T(8,128)(2,1)}) %all-gather.5.cloned.1.call-update) | async-done | bytes 4915216 | tf_op jit(solution)/shard_map/all_gather | solution.py:16
  66.9 11.3 %collective-permute-done = bf16[8,300,150]{1,0,2:T(8,128)(2,1)S(1)} collective-permute-done((bf16[8,300,150]{1,0,2:T(8,128)(2,1)}, bf16[8,300,150]{1,0,2:T(8,128)(2,1)S(1)}, u32[]{:S(2)}, u32[]{:S(2)}) %collective-permute-start) | collective-permute-done | bytes 720032 | tf_op jit(solution)/shard_map/ppermute | solution.py:36
  81.8 11.0 %collective-permute-done.1 = bf16[8,300,150]{1,0,2:T(8,128)(2,1)S(1)} collective-permute-done((bf16[8,300,150]{1,0,2:T(8,128)(2,1)S(1)}, bf16[8,300,150]{1,0,2:T(8,128)(2,1)S(1)}, u32[]{:S(2)}, u32[]{:S(2)}) %collective-permute-start.1) | collective-permute-done | bytes 720032 | tf_op jit(solution)/shard_map/ppermute | solution.py:36
  96.5 11.0 %collective-permute-done.2 = bf16[8,300,150]{1,0,2:T(8,128)(2,1)S(1)} collective-permute-done((bf16[8,300,150]{1,0,2:T(8,128)(2,1)S(1)}, bf16[8,300,150]{1,0,2:T(8,128)(2,1)S(1)}, u32[]{:S(2)}, u32[]{:S(2)}) %collective-permute-start.2) | collective-permute-done | bytes 720032 | tf_op jit(solution)/shard_map/ppermute | solution.py:36
  112.1 11.0 %collective-permute-done.3 = bf16[8,300,150]{1,0,2:T(8,128)(2,1)S(1)} collective-permute-done((bf16[8,300,150]{1,0,2:T(8,128)(2,1)S(1)}, bf16[8,300,150]{1,0,2:T(8,128)(2,1)S(1)}, u32[]{:S(2)}, u32[]{:S(2)}) %collective-permute-start.3) | collective-permute-done | bytes 720032 | tf_op jit(solution)/shard_map/ppermute | solution.py:36
  127.7 11.0 %collective-permute-done.4 = bf16[8,300,150]{1,0,2:T(8,128)(2,1)} collective-permute-done((bf16[8,300,150]{1,0,2:T(8,128)(2,1)S(1)}, bf16[8,300,150]{1,0,2:T(8,128)(2,1)}, u32[]{:S(2)}, u32[]{:S(2)}) %collective-permute-start.4) | collective-permute-done | bytes 720032 | tf_op jit(solution)/shard_map/ppermute | solution.py:36
  142.5 7.1 copy.37
  157.4 138.6 %all-gather.9.cloned.1.call-done = bf16[4,300,8192]{2,1,0:T(8,128)(2,1)} async-done(((bf16[1,300,8192]{2,1,0:T(8,128)(2,1)}), bf16[4,300,8192]{2,1,0:T(8,128)(2,1)}) %all-gather.9.cloned.1.call-update) | async-done | bytes 19660816 | tf_op jit(solution)/shard_map/all_gather | solution.py:17
  296.0 19.7 %reshape.49 = bf16[1200,8192]{1,0:T(8,128)(2,1)} reshape(bf16[4,300,8192]{2,1,0:T(8,128)(2,1)} %all-gather.9.cloned.1.call-done) | data formatting | bytes 39321600
  318.4 6.8 fusion.21
  325.2 6.8 fusion.23
  332.0 6.4 fusion.25
  338.3 6.4 fusion.27
  344.8 6.4 fusion.29
  357.5 23.0 %fusion.9 = bf16[8,300,1024]{2,1,0:T(8,128)(2,1)} fusion(f32[1024,8,300]{0,2,1:T(8,128)} %fusion.21, f32[1024,8,300]{0,2,1:T(8,128)} %fusion.23, f32[1024,8,300]{0,2,1:T(8,128)} %fusion.25, f32[1024,8,300]{0,2,1:T(8,128)} %fusion.27, f32[1024,8,300]{0,2,1:T(8,128)} %fusion.29, f32[1024,8,300]{0,2,1:T(8,128)S(1)} %fusion.33, f32[1024,8,300]{0,2,1:T(8,128)} %fusion.31, ...), kind=kOutput, calls=%fused_computation.8 | convolution fusion | flops 756940800 | bytes 75747336 | tf_op jit(solution)/shard_map/ons,sh->onh/dot_general | solution.py:44
  380.5 8.6 copy.48
  394.7 6.7 convert_bitcast_fusion
  401.4 8.7 copy.38
  410.1 8.9 copy.39
  419.0 19.5 %reshape.58 = bf16[1200,8192,1]{1,0,2:T(8,128)(2,1)} reshape(bf16[4,300,8192]{2,1,0:T(8,128)(2,1)} %all-gather.9.cloned.1.call-done) | data formatting | bytes 39321600
  438.4 26.2 %all-to-all-done.1 = bf16[8,300,1024]{1,0,2:T(8,128)(2,1)} async-done(((bf16[8,300,1024]{1,0,2:T(8,128)(2,1)}), bf16[8,300,1024]{1,0,2:T(8,128)(2,1)}, u32[]{:S(2)}, u32[]{:S(2)}) %all-to-all-start.1) | async-done | bytes 4915232 | tf_op jit(solution)/shard_map/all_to_all | solution.py:57
  464.7 12.8 %copy.61 = bf16[8,300,4,256]{3,2,0,1:T(4,128)(2,1)} copy(bf16[8,300,4,256]{1,0,3,2:T(8,128)(2,1)} %bitcast.13) | data formatting | bytes 9830400 | tf_op jit(solution)/shard_map/all_to_all | solution.py:57
  482.7 53.5 %fusion.64 = bf16[8,8192,256]{1,2,0:T(8,128)(2,1)} fusion(f32[8192,256]{0,1:T(8,128)} %copy.39, bf16[1200,8192,1]{1,0,2:T(8,128)(2,1)} %reshape.58, bf16[8,1200,256]{2,0,1:T(8,128)(2,1)} %bitcast.71), kind=kOutput, calls=%fused_computation.1.clone.clone.clone.clone.clone.clone.1 | convolution fusion | flops 40298872832 | bytes 66519040 | tf_op jit(solution)/shard_map/cp,icq->ipq/dot_general | solution.py:54
  536.2 51.8 %fusion.12 = bf16[8,1200,256]{2,1,0:T(8,128)(2,1)} fusion(bf16[1200,8192,1]{1,0,2:T(8,128)(2,1)} %reshape.58, bf16[8,8192,256]{1,2,0:T(8,128)(2,1)} %fusion.64), kind=kOutput, calls=%fused_computation.10 | convolution fusion | flops 40267776000 | bytes 58130432 | tf_op jit(solution)/shard_map/ap,ipq->iaq/dot_general | solution.py:61
  587.9 8.8 copy.53
  596.8 57.8 %all_to_all.49 = bf16[8,1200,256]{2,0,1:T(8,128)(2,1)S(1)} all-to-all(bf16[8,1200,256]{2,0,1:T(8,128)(2,1)S(1)} %copy.53), channel_id=1, replica_groups=mesh['vpair'=4,'rank'=8] {'vpair'}, dimensions={1} | all-to-all | bytes 9830400 | tf_op jit(solution)/shard_map/all_to_all | solution.py:64
  655.3 10.7 %fusion.17 = f32[8,300,1200]{2,0,1:T(8,128)} fusion(bf16[8,300,1024]{2,0,1:T(8,128)(2,1)S(1)} %bitcast.70, bf16[1200,8192]{1,0:T(8,128)(2,1)} %reshape.49, s32[]{:T(128)S(6)} %select_n.83), kind=kOutput, calls=%fused_computation.11 | convolution fusion | flops 5898240000 | bytes 18892804 | tf_op jit(solution)/shard_map/iaq,bq->iab/dot_general | solution.py:65
  666.0 14.2 %copy.56 = f32[8,300,1200]{1,0,2:T(8,128)} copy(f32[8,300,1200]{2,0,1:T(8,128)} %fusion.17) | data formatting | bytes 23040000 | tf_op jit(solution)/shard_map/iaq,bq->iab/dot_general | solution.py:65
  686.5 142.5 %reduce-scatter.2.cloned.1.call-done = f32[8,300,150]{1,0,2:T(8,128)} async-done(((f32[8,300,1200]{1,0,2:T(8,128)}), f32[8,300,150]{1,0,2:T(8,128)}) %reduce-scatter.2.cloned.1.call-update) | async-done | bytes 1440016 | tf_op jit(solution)/shard_map/reduce_scatter | solution.py:71
  833.4 43.4 %psum.7 = f32[]{:T(128)} all-reduce(f32[]{:T(128)} %get-tuple-element.10), channel_id=1, replica_groups=mesh['vpair'=4,'rank'=8] {'vpair','rank'}, use_global_device_ids=true, to_apply=%region_2.3 | all-reduce | flops 1 | bytes 8 | tf_op jit(solution)/shard_map/psum | solution.py:78
  877.4 90.0 %all-gather.7.cloned.1.call-done = f32[8,300,1200]{1,0,2:T(8,128)} async-done(((f32[8,300,150]{1,0,2:T(8,128)}), f32[8,300,1200]{1,0,2:T(8,128)}) %all-gather.7.cloned.1.call-update) | async-done | bytes 11520016 | tf_op jit(solution)/shard_map/all_gather | solution.py:79
  967.4 14.7 %copy.57 = f32[8,300,1200]{2,0,1:T(8,128)} copy(f32[8,300,1200]{1,0,2:T(8,128)} %all-gather.7.cloned.1.call-done) | data formatting | bytes 23040000
  (42 shorter events, 60.9 us)
Async XLA Ops:
  7.2 58.9 %all-gather.5.cloned.1.call-start = ((), (), s32[]{:S(2)}) async-start(), calls=%async_computation.4 | async-start | bytes 5603328 | tf_op jit(solution)/shard_map/all_gather | solution.py:16
  7.9 288.1 %all-gather.9.cloned.1.call-start = ((), (), s32[]{:S(2)}) async-start(), calls=%async_computation.7 | async-start | bytes 24903680 | tf_op jit(solution)/shard_map/all_gather | solution.py:17
  66.1 12.1 %collective-permute-start = (bf16[8,300,150]{1,0,2:T(8,128)(2,1)}, bf16[8,300,150]{1,0,2:T(8,128)(2,1)S(1)}, u32[]{:S(2)}, u32[]{:S(2)}) collective-permute-start(bf16[8,300,150]{1,0,2:T(8,128)(2,1)} %param.6), channel_id=1, source_target_pairs={{0,7},{1,0},{2,1},{3,2},{4,3},{5,4},{6,5},{7,6},{8,15},{9,8},{10,9... | collective-permute-start | bytes 2160008 | tf_op jit(solution)/shard_map/ppermute | solution.py:36
  78.2 14.6 %collective-permute-start.1 = (bf16[8,300,150]{1,0,2:T(8,128)(2,1)S(1)}, bf16[8,300,150]{1,0,2:T(8,128)(2,1)S(1)}, u32[]{:S(2)}, u32[]{:S(2)}) collective-permute-start(bf16[8,300,150]{1,0,2:T(8,128)(2,1)S(1)} %collective-permute-done), channel_id=1, source_target_pairs={{0,7},{1,0},{2,1},{3,2},{4,3},{5,4},{6,5},{7,6},{8,15},{9,8},{10,9... | collective-permute-start | bytes 2160008 | tf_op jit(solution)/shard_map/ppermute | solution.py:36
  92.8 14.7 %collective-permute-start.2 = (bf16[8,300,150]{1,0,2:T(8,128)(2,1)S(1)}, bf16[8,300,150]{1,0,2:T(8,128)(2,1)S(1)}, u32[]{:S(2)}, u32[]{:S(2)}) collective-permute-start(bf16[8,300,150]{1,0,2:T(8,128)(2,1)S(1)} %collective-permute-done.1), channel_id=1, source_target_pairs={{0,7},{1,0},{2,1},{3,2},{4,3},{5,4},{6,5},{7,6},{8,15},{9,8},{10,9... | collective-permute-start | bytes 2160008 | tf_op jit(solution)/shard_map/ppermute | solution.py:36
  107.4 1.0 copy-start.1
  108.4 14.7 %collective-permute-start.3 = (bf16[8,300,150]{1,0,2:T(8,128)(2,1)S(1)}, bf16[8,300,150]{1,0,2:T(8,128)(2,1)S(1)}, u32[]{:S(2)}, u32[]{:S(2)}) collective-permute-start(bf16[8,300,150]{1,0,2:T(8,128)(2,1)S(1)} %collective-permute-done.2), channel_id=1, source_target_pairs={{0,7},{1,0},{2,1},{3,2},{4,3},{5,4},{6,5},{7,6},{8,15},{9,8},{10,9... | collective-permute-start | bytes 2160008 | tf_op jit(solution)/shard_map/ppermute | solution.py:36
  123.1 0.9 copy-start.3
  124.0 14.7 %collective-permute-start.4 = (bf16[8,300,150]{1,0,2:T(8,128)(2,1)S(1)}, bf16[8,300,150]{1,0,2:T(8,128)(2,1)}, u32[]{:S(2)}, u32[]{:S(2)}) collective-permute-start(bf16[8,300,150]{1,0,2:T(8,128)(2,1)S(1)} %collective-permute-done.3), channel_id=1, source_target_pairs={{0,7},{1,0},{2,1},{3,2},{4,3},{5,4},{6,5},{7,6},{8,15},{9,8},{10,9... | collective-permute-start | bytes 2160008 | tf_op jit(solution)/shard_map/ppermute | solution.py:36
  138.6 15.9 %collective-permute-start.5 = (bf16[8,300,150]{1,0,2:T(8,128)(2,1)}, bf16[8,300,150]{1,0,2:T(8,128)(2,1)}, u32[]{:S(2)}, u32[]{:S(2)}) collective-permute-start(bf16[8,300,150]{1,0,2:T(8,128)(2,1)} %collective-permute-done.4), channel_id=1, source_target_pairs={{0,7},{1,0},{2,1},{3,2},{4,3},{5,4},{6,5},{7,6},{8,15},{9,8},{10,9... | collective-permute-start | bytes 2160008 | tf_op jit(solution)/shard_map/ppermute | solution.py:36
  149.5 239.5 %all-to-all-start = ((bf16[2048,4,256]{0,2,1:T(8,128)(2,1)}), bf16[2048,4,256]{0,2,1:T(8,128)(2,1)}, u32[]{:S(2)}, u32[]{:S(2)}) async-start(bf16[2048,4,256]{0,2,1:T(8,128)(2,1)} %bitcast.68), calls=%async_computation | async-start | bytes 8388608 | tf_op jit(solution)/shard_map/all_to_all | solution.py:51
  154.5 161.3 %copy-start = (bf16[8,300,150]{1,0,2:T(8,128)(2,1)S(1)}, bf16[8,300,150]{1,0,2:T(8,128)(2,1)}, u32[]{:S(2)}) copy-start(bf16[8,300,150]{1,0,2:T(8,128)(2,1)} %param.6) | copy-start | bytes 2160004
  154.5 203.0 %collective-permute-start.6 = (bf16[8,300,150]{1,0,2:T(8,128)(2,1)}, bf16[8,300,150]{1,0,2:T(8,128)(2,1)}, u32[]{:S(2)}, u32[]{:S(2)}) collective-permute-start(bf16[8,300,150]{1,0,2:T(8,128)(2,1)} %collective-permute-done.5), channel_id=1, source_target_pairs={{0,7},{1,0},{2,1},{3,2},{4,3},{5,4},{6,5},{7,6},{8,15},{9,8},{10,9... | collective-permute-start | bytes 2160008 | tf_op jit(solution)/shard_map/ppermute | solution.py:36
  325.2 6.8 copy-start.4
  332.0 6.4 copy-start.2
  389.0 75.6 %all-to-all-start.1 = ((bf16[8,300,1024]{1,0,2:T(8,128)(2,1)}), bf16[8,300,1024]{1,0,2:T(8,128)(2,1)}, u32[]{:S(2)}, u32[]{:S(2)}) async-start(bf16[8,300,1024]{1,0,2:T(8,128)(2,1)} %copy.48), calls=%async_computation.1 | async-start | bytes 12582912 | tf_op jit(solution)/shard_map/all_to_all | solution.py:57
  394.7 434.4 %reduce-scatter.2.cloned.1.call-start = ((), (), s32[]{:S(2)}) async-start(), calls=%async_computation.5 | async-start | bytes 16588800 | tf_op jit(solution)/shard_map/reduce_scatter | solution.py:71
  680.2 148.9 %copy-start.5 = (f32[8]{0:T(128)S(1)}, f32[8]{0:T(128)}, u32[]{:S(2)}) copy-start(f32[8]{0:T(128)} %param.11) | copy-start | bytes 100
  680.2 287.3 %all-gather.7.cloned.1.call-start = ((), (), s32[]{:S(2)}) async-start(), calls=%async_computation.6 | async-start | bytes 16588800 | tf_op jit(solution)/shard_map/all_gather | solution.py:79
Sparse Core Ops, SparseCore 0:
  9.6 56.4 all-gather.4
  67.9 228.0 all-gather.8
  680.3 148.6 reduce-scatter.1
  833.5 133.9 all-gather.6
